TPU v7x, 32 devices: a whole 2x2x4 slice. The times are simulated.
32 devices in a mesh: shard: 2 (over x), rep: 16 (over z, y, core).
Axes of the slice: x: 2, y: 2, z: 4, core: 2. Of those that a mesh axis runs over, the one named last changes fastest.
Arguments:
- frames_in: bfloat16 [16, 1500, 384], P('rep', 'shard'), may hold values from -6 to 6
- params: bfloat16 [2, 1774080], P(None, 'shard'), may hold values from -8 to 8
- moment_one: float32 [2, 1774080], P(None, 'shard'), may hold values from -170.41127 to 170.41127
- moment_two: float32 [2, 1774080], P(None, 'shard'), may hold values from 14.4 to 4800
- cotangent: bfloat16 [16, 1500, 384], P('rep', 'shard'), may hold values from -6 to 6
Outputs:
- encoded: bfloat16 [16, 1500, 384], P('rep', 'shard')
- frames_grad: bfloat16 [16, 1500, 384], P('rep', 'shard')
- param_grad: float32 [2, 1774080], P(None, 'shard')
- new_params: float32 [2, 1774080], P(None, 'shard')
- new_one: float32 [2, 1774080], P(None, 'shard')
- new_two: float32 [2, 1774080], P(None, 'shard')
All inputs are finite; a program needn't handle non-finite values.
Results may differ from a plain program's by a relative error of at most 0.019.
Values may be sent and summed in bfloat16 or wider, within the bound.
A program may use at most 384 MiB of HBM per device.

v0:
```python
from functools import partial

import jax
import jax.numpy as jnp
from jax import lax
from jax.sharding import PartitionSpec as P

D = 384
HEADS = 6
FF = 1536
LAYERS = 2


ln_eps = 1e-05
rate = 0.01
beta_one = 0.9
beta_two = 0.95
adam_eps = 1e-08
decay = 0.1
fix_one = 1.0 - 0.9**3
fix_two = 1.0 - 0.95**3


def unpack(vector):
    lengths = [D * 3 * D, D * D, D * FF, FF * D, 2 * D, 6 * D, FF]
    shapes = [(D, 3 * D), (D, D), (D, FF), (FF, D), (2, D), (6, D), (FF,)]
    pieces = []
    offset = 0
    for length, shape_of in zip(lengths, shapes):
        pieces.append(vector[offset : offset + length].reshape(shape_of))
        offset += length
    return pieces


def normalize(values, gain, shift):
    center = values - jnp.mean(values, axis=-1, keepdims=True)
    spread = jnp.mean(center * center, axis=-1, keepdims=True)
    return center * lax.rsqrt(spread + ln_eps) * gain + shift


def matmul(left, right):
    return jnp.dot(left, right, preferred_element_type=jnp.float32)


def inner_rows(left, right):
    return lax.dot_general(
        left, right, (((0,), (0,)), ((), ())), preferred_element_type=jnp.float32
    )


def outer_cols(left, right):
    return lax.dot_general(
        left, right, (((1,), (1,)), ((), ())), preferred_element_type=jnp.float32
    )


def attend(inputs):
    query_low, key_low, value_low = inputs
    row_count = query_low.shape[0]
    head = D // HEADS
    query_h = query_low.reshape(row_count, HEADS, head)
    key_h = key_low.reshape(-1, HEADS, head)
    value_h = value_low.reshape(-1, HEADS, head)
    scores = jnp.einsum("qhd,khd->hqk", query_h, key_h, preferred_element_type=jnp.float32) * 0.125
    row_max = jnp.max(scores, axis=-1, keepdims=True)
    exp_scores = jnp.exp(scores - row_max)
    row_total = jnp.sum(exp_scores, axis=-1, keepdims=True)
    prob_low = (exp_scores / row_total).astype(jnp.bfloat16)
    mixed = jnp.einsum("hqk,khd->qhd", prob_low, value_h, preferred_element_type=jnp.float32)
    return (mixed.reshape(row_count, D), (row_max + jnp.log(row_total))[..., 0])


def attend_back(inputs):
    query_low, key_low, value_low, log_total, grad_low = inputs
    row_count = query_low.shape[0]
    head = D // HEADS
    query_h = query_low.reshape(row_count, HEADS, head)
    key_h = key_low.reshape(-1, HEADS, head)
    value_h = value_low.reshape(-1, HEADS, head)
    grad_h = grad_low.reshape(row_count, HEADS, head)
    scores = jnp.einsum("qhd,khd->hqk", query_h, key_h, preferred_element_type=jnp.float32) * 0.125
    probs = jnp.exp(scores - log_total[..., None])
    prob_low = probs.astype(jnp.bfloat16)
    value_grad = jnp.einsum("hqk,qhd->khd", prob_low, grad_h, preferred_element_type=jnp.float32)
    prob_grad = jnp.einsum("qhd,khd->hqk", grad_h, value_h, preferred_element_type=jnp.float32)
    score_grad = (probs * (prob_grad - jnp.sum(probs * prob_grad, axis=-1, keepdims=True))).astype(
        jnp.bfloat16
    )
    query_grad = (
        jnp.einsum("hqk,khd->qhd", score_grad, key_h, preferred_element_type=jnp.float32) * 0.125
    )
    key_grad = (
        jnp.einsum("hqk,qhd->khd", score_grad, query_h, preferred_element_type=jnp.float32) * 0.125
    )
    return (query_grad.reshape(row_count, D), key_grad.reshape(-1, D), value_grad.reshape(-1, D))


def layer_forward(stream, weights, clip_count, rows_dev):
    qkv_w, out_w, up_w, down_w, gain_rows, shift_rows, up_bias = weights
    gain_rows = gain_rows.astype(jnp.float32)
    shift_rows = shift_rows.astype(jnp.float32)
    up_bias = up_bias.astype(jnp.float32)
    normed_low = normalize(stream, gain_rows[0], shift_rows[0]).astype(jnp.bfloat16)
    qkv = matmul(normed_low, qkv_w)
    query_low = (qkv[:, :D] + shift_rows[1]).astype(jnp.bfloat16)
    key_low = qkv[:, D : 2 * D].astype(jnp.bfloat16)
    value_low = (qkv[:, 2 * D :] + shift_rows[2]).astype(jnp.bfloat16)
    keys_all, values_all = (
        lax.all_gather(key_low.reshape(clip_count, rows_dev, D), "shard", axis=1, tiled=True),
        lax.all_gather(value_low.reshape(clip_count, rows_dev, D), "shard", axis=1, tiled=True),
    )
    mixed, log_total = lax.map(
        attend, (query_low.reshape(clip_count, rows_dev, D), keys_all, values_all)
    )
    mixed_low = mixed.reshape(-1, D).astype(jnp.bfloat16)
    middle = stream + matmul(mixed_low, out_w) + shift_rows[3]
    normed_two = normalize(middle, gain_rows[1], shift_rows[4]).astype(jnp.bfloat16)
    pre_act = matmul(normed_two, up_w) + up_bias
    hidden_low = jax.nn.gelu(pre_act, approximate=False).astype(jnp.bfloat16)
    result = middle + matmul(hidden_low, down_w) + shift_rows[5]
    kept_vals = (
        stream,
        normed_low,
        query_low,
        keys_all,
        values_all,
        log_total,
        mixed_low,
        middle,
        normed_two,
        pre_act,
        hidden_low,
    )
    return (kept_vals, result)


def layer_backward(grad_out, weights, kept_vals, clip_count, rows_dev):
    qkv_w, out_w, up_w, down_w, gain_rows, shift_rows, up_bias = weights
    gain_rows = gain_rows.astype(jnp.float32)
    shift_rows = shift_rows.astype(jnp.float32)
    (
        stream,
        normed_low,
        query_low,
        keys_all,
        values_all,
        log_total,
        mixed_low,
        middle,
        normed_two,
        pre_act,
        hidden_low,
    ) = kept_vals
    branch_low = grad_out.astype(jnp.bfloat16)
    down_grad = inner_rows(hidden_low, branch_low)
    down_shift_grad = jnp.sum(branch_low.astype(jnp.float32), axis=0)
    hidden_grad = outer_cols(branch_low, down_w)
    gelu_out, gelu_back = jax.vjp(partial(jax.nn.gelu, approximate=False), pre_act)
    pre_low = gelu_back(hidden_grad)[0].astype(jnp.bfloat16)
    up_grad = inner_rows(normed_two, pre_low)
    up_shift_grad = jnp.sum(pre_low.astype(jnp.float32), axis=0)
    normed_grad = outer_cols(pre_low, up_w)
    norm_out, norm_back = jax.vjp(normalize, middle, gain_rows[1], shift_rows[4])
    middle_in, gain_two_grad, shift_two_grad = norm_back(normed_grad)
    middle_grad = grad_out + middle_in
    attn_low = middle_grad.astype(jnp.bfloat16)
    out_grad = inner_rows(mixed_low, attn_low)
    out_shift_grad = jnp.sum(attn_low.astype(jnp.float32), axis=0)
    mixed_grad = outer_cols(attn_low, out_w).astype(jnp.bfloat16)
    query_grad, key_part, value_part = lax.map(
        attend_back,
        (
            query_low.reshape(clip_count, rows_dev, D),
            keys_all,
            values_all,
            log_total,
            mixed_grad.reshape(clip_count, rows_dev, D),
        ),
    )
    key_grad, value_grad = (
        lax.psum_scatter(
            key_part.astype(jnp.bfloat16), "shard", scatter_dimension=1, tiled=True
        ).astype(jnp.float32),
        lax.psum_scatter(
            value_part.astype(jnp.bfloat16), "shard", scatter_dimension=1, tiled=True
        ).astype(jnp.float32),
    )
    qkv_low = jnp.concatenate(
        [
            query_grad.reshape(-1, D).astype(jnp.bfloat16),
            key_grad.reshape(-1, D).astype(jnp.bfloat16),
            value_grad.reshape(-1, D).astype(jnp.bfloat16),
        ],
        axis=1,
    )
    qkv_grad = inner_rows(normed_low, qkv_low)
    column_sums = jnp.sum(qkv_low.astype(jnp.float32), axis=0)
    first_grad = outer_cols(qkv_low, qkv_w)
    norm_out_one, norm_back_one = jax.vjp(normalize, stream, gain_rows[0], shift_rows[0])
    stream_in, gain_one_grad, shift_one_grad = norm_back_one(first_grad)
    grad_in = middle_grad + stream_in
    flat_grad = jnp.concatenate(
        [
            qkv_grad.reshape(-1),
            out_grad.reshape(-1),
            up_grad.reshape(-1),
            down_grad.reshape(-1),
            gain_one_grad,
            gain_two_grad,
            shift_one_grad,
            column_sums[:D],
            column_sums[2 * D :],
            out_shift_grad,
            shift_two_grad,
            down_shift_grad,
            up_shift_grad,
        ]
    )
    return (grad_in, flat_grad)


def body(frames_in, params, moment_one, moment_two, cotangent):
    clip_count, rows_dev, width = frames_in.shape
    stream = frames_in.astype(jnp.float32).reshape(-1, width)
    kept_layers = []
    for layer_no in range(LAYERS):
        full_vector = lax.all_gather(params[layer_no], "shard", axis=0, tiled=True)
        weights = unpack(full_vector)
        kept_vals, stream = layer_forward(stream, weights, clip_count, rows_dev)
        kept_layers.append((weights, kept_vals))
    encoded = stream.astype(jnp.bfloat16).reshape(clip_count, rows_dev, width)
    grad_stream = cotangent.astype(jnp.float32).reshape(-1, width)
    layer_grads = [None] * LAYERS
    for layer_no in reversed(range(LAYERS)):
        weights = unpack(lax.all_gather(params[layer_no], "shard", axis=0, tiled=True))
        grad_stream, flat_grad = layer_backward(
            grad_stream, weights, kept_layers[layer_no][1], clip_count, rows_dev
        )
        group_part = lax.psum_scatter(
            flat_grad.astype(jnp.bfloat16), "shard", scatter_dimension=0, tiled=True
        ).astype(jnp.float32)
        layer_grads[layer_no] = lax.psum(group_part, "rep")
    stacked = jnp.stack(layer_grads)
    frames_grad = grad_stream.astype(jnp.bfloat16).reshape(clip_count, rows_dev, width)
    old_values = params.astype(jnp.float32)
    new_one = beta_one * moment_one + (1.0 - beta_one) * stacked
    new_two = beta_two * moment_two + (1.0 - beta_two) * stacked * stacked
    step_size = new_one / fix_one / (jnp.sqrt(new_two / fix_two) + adam_eps) + decay * old_values
    new_params = old_values - rate * step_size
    return (encoded, frames_grad, stacked, new_params, new_one, new_two)


def solution(mesh):
    in_specs = (
        P("rep", "shard", None),
        P(None, "shard"),
        P(None, "shard"),
        P(None, "shard"),
        P("rep", "shard", None),
    )
    out_specs = (
        P("rep", "shard", None),
        P("rep", "shard", None),
        P(None, "shard"),
        P(None, "shard"),
        P(None, "shard"),
        P(None, "shard"),
    )
    return jax.shard_map(body, mesh=mesh, in_specs=in_specs, out_specs=out_specs, check_vma=False)
```

profile of v0, /device:TPU:1, one launch (start us, length us, event | category | flops | bytes accessed | tf_op | source)
XLA Modules:
  0.0 1166.6 jit_solution(15289688087438336875)
XLA Ops:
  7.2 8.7 fusion.103
  17.6 89.8 %all-gather.17.cloned.1.call-done = bf16[1,1774080]{1,0:T(2,128)(2,1)} async-done(((bf16[1,887040]{1,0:T(2,128)(2,1)}), bf16[1,1774080]{1,0:T(2,128)(2,1)}) %all-gather.17.cloned.1.call-update) | async-done | bytes 3548176 | tf_op jit(solution)/shard_map/all_gather | solution.py:227
  107.4 15.8 %slice_reduce_fusion.5 = bf16[442368]{0:T(1024)(128)(2,1)S(1)} fusion(bf16[1,1774080]{1,0:T(2,128)(2,1)} %all-gather.17.cloned.1.call-done), kind=kLoop, calls=%fused_computation.81 | loop fusion | bytes 1769472 | tf_op jit(solution)/shard_map/slice | solution.py:30
  133.2 26.6 %slice_reduce_fusion.2 = (bf16[589824]{0:T(1024)(128)(2,1)S(1)}, bf16[589824]{0:T(1024)(128)(2,1)S(1)}) fusion(bf16[1,1774080]{1,0:T(2,128)(2,1)} %all-gather.17.cloned.1.call-done), kind=kLoop, calls=%fused_computation.76 | loop fusion | bytes 4718592 | tf_op jit(solution)/shard_map/slice | solution.py:30
  159.7 39.3 %all-gather.19.cloned.1.call-done = bf16[1,1774080]{1,0:T(2,128)(2,1)} async-done(((bf16[1,887040]{1,0:T(2,128)(2,1)}), bf16[1,1774080]{1,0:T(2,128)(2,1)}) %all-gather.19.cloned.1.call-update) | async-done | bytes 3548176 | tf_op jit(solution)/shard_map/all_gather | solution.py:227
  199.0 16.7 %slice_reduce_fusion.4 = bf16[442368]{0:T(1024)(128)(2,1)} fusion(bf16[1,1774080]{1,0:T(2,128)(2,1)} %all-gather.19.cloned.1.call-done), kind=kLoop, calls=%fused_computation.80 | loop fusion | bytes 1769472 | tf_op jit(solution)/shard_map/slice | solution.py:30
  215.7 6.3 slice_reduce_fusion.7
  233.4 3.6 copy.37
  238.0 10.1 all-gather.21.cloned.1.call-done
  248.1 4.7 copy.35
  256.2 11.2 multiply_reduce_fusion.3
  267.4 11.5 fusion
  279.0 11.9 %fusion.44 = bf16[6,64,750]{2,1,0:T(8,128)(2,1)S(1)} fusion(bf16[1500,6,64]{0,2,1:T(8,128)(2,1)S(1)} %reshape.543, f32[6,750,1500]{2,1,0:T(8,128)} %get-tuple-element.168, f32[6,750]{1,0:T(8,128)S(1)} %fusion, f32[6,750]{1,0:T(8,128)S(1)} %get-tuple-element.167), kind=kOutput, calls=%fused_computation.104 | convolution fusion | flops 891288000 | bytes 28764000 | tf_op jit(solution)/shard_map/while/body/eval_jaxpr/hqk,khd->qhd/dot_general | solution.py:69
  292.6 13.1 %multiply_convert_fusion.3 = (bf16[750,1536]{1,0:T(8,128)(2,1)S(1)}, f32[750,1536]{1,0:T(8,128)}, f32[750,1536]{1,0:T(8,128)}) fusion(f32[1536]{0:T(1024)S(1)} %fusion.70, bf16[384,1536]{1,0:T(8,128)(2,1)S(1)} %copy-done.46, f32[750,384]{1,0:T(8,128)S(1)} %get-tuple-element.170, f32[384]{0:T(512)S(1)} %get-tuple-element.120, ...), kind=kOutput, calls=%fused_computation.47 | convolution fusion | flops 962208000 | bytes 13866864 | tf_op jit(solution)/shard_map/dot_general | solution.py:42
  314.5 5.9 slice_reduce_fusion.6
  321.3 27.3 %slice_reduce_fusion = (bf16[589824]{0:T(1024)(128)(2,1)}, bf16[589824]{0:T(1024)(128)(2,1)S(1)}) fusion(bf16[1,1774080]{1,0:T(2,128)(2,1)} %all-gather.19.cloned.1.call-done), kind=kLoop, calls=%fused_computation.74 | loop fusion | bytes 4718592 | tf_op jit(solution)/shard_map/slice | solution.py:30
  355.9 4.9 copy.40
  364.2 5.0 copy.38
  369.1 4.2 reshape.548
  373.3 11.1 multiply_reduce_fusion.2
  384.5 11.6 fusion.1
  396.1 11.8 %fusion.43 = bf16[6,64,750]{2,1,0:T(8,128)(2,1)S(1)} fusion(bf16[1500,6,64]{0,2,1:T(8,128)(2,1)S(1)} %copy-done.18, f32[6,750,1500]{2,1,0:T(8,128)} %get-tuple-element.175, f32[6,750]{1,0:T(8,128)S(1)} %fusion.1, f32[6,750]{1,0:T(8,128)S(1)} %get-tuple-element.174), kind=kOutput, calls=%fused_computation.103 | convolution fusion | flops 891288000 | bytes 28764000 | tf_op jit(solution)/shard_map/while/body/eval_jaxpr/hqk,khd->qhd/dot_general | solution.py:69
  409.5 12.4 %multiply_convert_fusion.2 = (bf16[750,1536]{1,0:T(8,128)(2,1)}, f32[750,1536]{1,0:T(8,128)S(1)}, f32[750,1536]{1,0:T(8,128)S(1)}) fusion(f32[1536]{0:T(1024)S(1)} %fusion.69, bf16[384,1536]{1,0:T(8,128)(2,1)S(1)} %copy-done.50, f32[750,384]{1,0:T(8,128)S(1)} %get-tuple-element.177, f32[384]{0:T(512)S(1)} %copy-done.88, f32[384]{0:T(512)S(1)} %copy-done.70, ...), kind=kOutput, calls=%fused_computation.34 | convolution fusion | flops 962208000 | bytes 13866864 | tf_op jit(solution)/shard_map/dot_general | solution.py:42
  431.7 12.3 %fusion.27 = bf16[6,64,1500]{2,1,0:T(8,128)(2,1)} fusion(bf16[750,6,64]{0,2,1:T(8,128)(2,1)S(1)} %bitcast.174, f32[6,750,1500]{2,1,0:T(8,128)} %get-tuple-element.175, f32[6,750]{1,0:T(8,128)S(1)} %log_add_fusion.1), kind=kOutput, calls=%fused_computation.68 | convolution fusion | flops 884825984 | bytes 28746000 | tf_op jit(solution)/shard_map/while/body/eval_jaxpr/hqk,qhd->khd/dot_general | solution.py:84
  443.9 22.3 %multiply_reduce_fusion.1 = (f32[6,750]{1,0:T(8,128)S(1)}, f32[6,750,1500]{2,1,0:T(8,128)}) fusion(f32[6,750,1500]{2,1,0:T(8,128)} %get-tuple-element.175, f32[6,750]{1,0:T(8,128)S(1)} %log_add_fusion.1, bf16[750,6,64]{0,2,1:T(8,128)(2,1)S(1)} %bitcast.175, bf16[1500,6,64]{0,2,1:T(8,128)(2,1)} %reshape.548), kind=kOutput, calls=%fused_computation.4 | convolution fusion | flops 890995520 | bytes 55764000 | tf_op jit(solution)/shard_map/while/body/eval_jaxpr/qhd,khd->hqk/dot_general | solution.py:85
  466.3 22.8 %multiply_convert_fusion.1 = bf16[6,750,1500]{2,1,0:T(8,128)(2,1)} fusion(f32[6,750,1500]{2,1,0:T(8,128)} %get-tuple-element.181, f32[6,750,1500]{2,1,0:T(8,128)} %get-tuple-element.175, f32[6,750]{1,0:T(8,128)S(1)} %get-tuple-element.180, f32[6,750]{1,0:T(8,128)S(1)} %log_add_fusion.1), kind=kLoop, calls=%fused_computation.3 | loop fusion | flops 33750000 | bytes 67536000 | tf_op jit(solution)/shard_map/while/body/eval_jaxpr/convert_element_type | solution.py:86
  489.1 8.5 fusion.25
  501.0 4.2 convolution_convert_fusion.2
  508.3 4.1 convolution_convert_fusion.3
  518.9 10.3 fusion.41
  529.1 37.3 %all-reduce.21.cloned.1.call-done = (bf16[1,1500,384]{1,2,0:T(8,128)(2,1)}, bf16[1,1500,384]{1,2,0:T(8,128)(2,1)}) async-done(((bf16[1,1500,384]{1,2,0:T(8,128)(2,1)}, bf16[1,1500,384]{1,2,0:T(8,128)(2,1)}), (bf16[1,1500,384]{1,2,0:T(8,128)(2,1)}, bf16[1,1500,384]{1,2,0:T(8,128)(2,1)})) %all-reduce.21.cloned.1.call-update) | async-done | bytes 2304016
  569.5 3.7 multiply_reduce_fusion.5
  577.9 4.0 fusion.110
  588.3 12.3 %fusion.30 = bf16[6,64,1500]{2,1,0:T(8,128)(2,1)} fusion(bf16[750,6,64]{0,2,1:T(8,128)(2,1)S(1)} %bitcast.176, f32[6,750,1500]{2,1,0:T(8,128)} %get-tuple-element.168, f32[6,750]{1,0:T(8,128)S(1)} %log_add_fusion), kind=kOutput, calls=%fused_computation.69 | convolution fusion | flops 884825984 | bytes 28746000 | tf_op jit(solution)/shard_map/while/body/eval_jaxpr/hqk,qhd->khd/dot_general | solution.py:84
  600.6 22.2 %multiply_reduce_fusion = (f32[6,750]{1,0:T(8,128)S(1)}, f32[6,750,1500]{2,1,0:T(8,128)}) fusion(f32[6,750,1500]{2,1,0:T(8,128)} %get-tuple-element.168, f32[6,750]{1,0:T(8,128)S(1)} %log_add_fusion, bf16[750,6,64]{0,2,1:T(8,128)(2,1)S(1)} %bitcast.177, bf16[1500,6,64]{0,2,1:T(8,128)(2,1)} %copy-done.17), kind=kOutput, calls=%fused_computation.1 | convolution fusion | flops 890995520 | bytes 55764000 | tf_op jit(solution)/shard_map/while/body/eval_jaxpr/qhd,khd->hqk/dot_general | solution.py:85
  627.7 22.8 %multiply_convert_fusion = bf16[6,750,1500]{2,1,0:T(8,128)(2,1)} fusion(f32[6,750,1500]{2,1,0:T(8,128)} %get-tuple-element.185, f32[6,750,1500]{2,1,0:T(8,128)} %get-tuple-element.168, f32[6,750]{1,0:T(8,128)S(1)} %get-tuple-element.184, f32[6,750]{1,0:T(8,128)S(1)} %log_add_fusion), kind=kLoop, calls=%fused_computation | loop fusion | flops 33750000 | bytes 67536000 | tf_op jit(solution)/shard_map/while/body/eval_jaxpr/convert_element_type | solution.py:86
  650.4 8.6 fusion.26
  663.3 4.4 convolution_convert_fusion.4
  671.0 4.1 convolution_convert_fusion.5
  675.1 3.6 reshape.560
  696.4 9.1 fusion.42
  705.5 24.3 %all-reduce.19.cloned.1.call-done = (bf16[1,1500,384]{1,2,0:T(8,128)(2,1)}, bf16[1,1500,384]{1,2,0:T(8,128)(2,1)}) async-done(((bf16[1,1500,384]{1,2,0:T(8,128)(2,1)}, bf16[1,1500,384]{1,2,0:T(8,128)(2,1)}), (bf16[1,1500,384]{1,2,0:T(8,128)(2,1)}, bf16[1,1500,384]{1,2,0:T(8,128)(2,1)})) %all-reduce.19.cloned.1.call-update) | async-done | bytes 2304016
  761.0 170.1 %all-reduce.17.cloned.1.call-done = (bf16[1774080]{0:T(1024)(128)(2,1)}, bf16[1774080]{0:T(1024)(128)(2,1)}) async-done(((bf16[1774080]{0:T(1024)(128)(2,1)}, bf16[1774080]{0:T(1024)(128)(2,1)}), (bf16[1774080]{0:T(1024)(128)(2,1)}, bf16[1774080]{0:T(1024)(128)(2,1)})) %all-reduce.17.cloned.1.call-update) | async-done | bytes 7096336
  933.5 17.4 %stack.10 = f32[1,887040]{1,0:T(1,128)} reshape(f32[887040]{0:T(1024)S(1)} %dynamic-slice_convert_fusion) | data formatting | bytes 7096320 | tf_op jit(solution)/shard_map/stack | solution.py:243
  951.8 17.4 %stack.9 = f32[1,887040]{1,0:T(1,128)} reshape(f32[887040]{0:T(1024)S(1)} %dynamic-slice_convert_fusion.1) | data formatting | bytes 7096320 | tf_op jit(solution)/shard_map/stack | solution.py:243
  970.5 4.0 fusion.50
  976.1 145.8 %all-reduce.15.cloned.1.call-done = (f32[1,887040]{1,0:T(1,128)}, f32[1,887040]{1,0:T(1,128)}) async-done(((f32[1,887040]{1,0:T(1,128)}, f32[1,887040]{1,0:T(1,128)}), (f32[1,887040]{1,0:T(1,128)}, f32[1,887040]{1,0:T(1,128)})) %all-reduce.15.cloned.1.call-update) | async-done | bytes 7096336 | tf_op jit(solution)/shard_map/psum | solution.py:242
  1121.9 37.6 %convert_subtract_fusion = (f32[2,887040]{1,0:T(2,128)}, f32[2,887040]{1,0:T(2,128)}, f32[2,887040]{1,0:T(2,128)}, f32[2,887040]{1,0:T(2,128)}) fusion(bf16[2,887040]{1,0:T(2,128)(2,1)S(1)} %copy-done, f32[2,887040]{1,0:T(2,128)} %param.7, f32[2,887040]{1,0:T(2,128)} %param.8, f32[1,887040]{1,0:T(1,128)} %get-tuple-element.129, ...), kind=kLoop, calls=%fused_computation.21 | loop fusion | flops 30159360 | bytes 53222400 | tf_op jit(solution)/shard_map/sub | solution.py:249
  (379 shorter events, 152.8 us)
Async XLA Ops:
  7.2 100.3 %all-gather.17.cloned.1.call-start = ((), (), s32[]{:S(2)}) async-start(), calls=%async_computation | async-start | bytes 10644480 | tf_op jit(solution)/shard_map/all_gather | solution.py:227
  16.0 183.0 %all-gather.19.cloned.1.call-start = ((), (), s32[]{:S(2)}) async-start(), calls=%async_computation.1 | async-start | bytes 10644480 | tf_op jit(solution)/shard_map/all_gather | solution.py:227
  16.7 216.6 %all-gather.23.cloned.1.call-start = ((), (), s32[]{:S(2)}) async-start(), calls=%async_computation.3 | async-start | bytes 1732608 | tf_op jit(solution)/shard_map/all_gather | solution.py:109
  17.2 110.3 %copy-start.58 = (f32[750]{0:T(1024)}, f32[750]{0:T(1024)S(1)}, u32[]{:S(2)}) copy-start(f32[750]{0:T(1024)S(1)} %broadcast_multiply_fusion.3) | copy-start | bytes 9004
  17.6 89.9 %copy-start.77 = (f32[750]{0:T(1024)}, f32[750]{0:T(1024)S(1)}, u32[]{:S(2)}) copy-start(f32[750]{0:T(1024)S(1)} %fusion.54) | copy-start | bytes 9004
  17.6 110.0 %copy-start.63 = (f32[750]{0:T(1024)}, f32[750]{0:T(1024)S(1)}, u32[]{:S(2)}) copy-start(f32[750]{0:T(1024)S(1)} %fusion.71) | copy-start | bytes 9004
  126.3 166.3 %copy-start.68 = (f32[384]{0:T(512)}, f32[384]{0:T(512)S(1)}, u32[]{:S(2)}) copy-start(f32[384]{0:T(512)S(1)} %get-tuple-element.192) | copy-start | bytes 4612
  126.3 166.3 %copy-start.86 = (f32[384]{0:T(512)}, f32[384]{0:T(512)S(1)}, u32[]{:S(2)}) copy-start(f32[384]{0:T(512)S(1)} %get-tuple-element.120) | copy-start | bytes 4612
  130.2 117.9 %all-gather.21.cloned.1.call-start = ((), (), s32[]{:S(2)}) async-start(), calls=%async_computation.2 | async-start | bytes 1732608 | tf_op jit(solution)/shard_map/all_gather | solution.py:110
  133.1 222.7 %all-gather.27.cloned.1.call-start = ((), (), s32[]{:S(2)}) async-start(), calls=%async_computation.5 | async-start | bytes 1732608 | tf_op jit(solution)/shard_map/all_gather | solution.py:109
  230.6 25.7 %copy-start.19 = (bf16[750,384]{0,1:T(8,128)(2,1)}, bf16[750,384]{0,1:T(8,128)(2,1)S(1)}, u32[]{:S(2)}) copy-start(bf16[750,384]{0,1:T(8,128)(2,1)S(1)} %copy.36) | copy-start | bytes 1728004
  231.3 61.3 %copy-start.96 = (f32[1536]{0:T(1024)}, f32[1536]{0:T(1024)S(1)}, u32[]{:S(2)}) copy-start(f32[1536]{0:T(1024)S(1)} %fusion.70) | copy-start | bytes 18436
  233.4 74.3 %copy-start.89 = (f32[384]{0:T(512)}, f32[384]{0:T(512)S(1)}, u32[]{:S(2)}) copy-start(f32[384]{0:T(512)S(1)} %get-tuple-element.193) | copy-start | bytes 4612
  233.4 74.3 %copy-start.94 = (f32[384]{0:T(512)}, f32[384]{0:T(512)S(1)}, u32[]{:S(2)}) copy-start(f32[384]{0:T(512)S(1)} %get-tuple-element.109) | copy-start | bytes 4612
  238.0 29.4 %copy-start.6 = (bf16[1500,6,64]{0,2,1:T(8,128)(2,1)}, bf16[1500,6,64]{0,2,1:T(8,128)(2,1)S(1)}, u32[]{:S(2)}) copy-start(bf16[1500,6,64]{0,2,1:T(8,128)(2,1)S(1)} %reshape.546) | copy-start | bytes 3456004
  256.2 22.8 %copy-start.17 = (bf16[1500,6,64]{0,2,1:T(8,128)(2,1)}, bf16[1500,6,64]{0,2,1:T(8,128)(2,1)S(1)}, u32[]{:S(2)}) copy-start(bf16[1500,6,64]{0,2,1:T(8,128)(2,1)S(1)} %reshape.543) | copy-start | bytes 3456004
  290.9 14.8 %copy-start.38 = (bf16[6,64,750]{2,1,0:T(8,128)(2,1)}, bf16[6,64,750]{2,1,0:T(8,128)(2,1)S(1)}, u32[]{:S(2)}) copy-start(bf16[6,64,750]{2,1,0:T(8,128)(2,1)S(1)} %fusion.44) | copy-start | bytes 1728004
  291.6 14.2 %copy-start.4 = (f32[750,384]{1,0:T(8,128)}, f32[750,384]{1,0:T(8,128)S(1)}, u32[]{:S(2)}) copy-start(f32[750,384]{1,0:T(8,128)S(1)} %get-tuple-element.170) | copy-start | bytes 3456004
  291.6 14.1 %copy-start.56 = (f32[750]{0:T(1024)}, f32[750]{0:T(1024)S(1)}, u32[]{:S(2)}) copy-start(f32[750]{0:T(1024)S(1)} %broadcast_multiply_fusion.2) | copy-start | bytes 9004
  291.9 13.8 %copy-start.60 = (f32[750]{0:T(1024)}, f32[750]{0:T(1024)S(1)}, u32[]{:S(2)}) copy-start(f32[750]{0:T(1024)S(1)} %fusion.72) | copy-start | bytes 9004
  311.6 52.6 %all-gather.25.cloned.1.call-start = ((), (), s32[]{:S(2)}) async-start(), calls=%async_computation.4 | async-start | bytes 1732608 | tf_op jit(solution)/shard_map/all_gather | solution.py:110
  314.5 252.0 %all-reduce.21.cloned.1.call-start = ((), (), s32[]{:S(2)}) async-start(), calls=%async_computation.9 | async-start | bytes 4718592
  355.8 17.5 %copy-start.21 = (bf16[750,384]{0,1:T(8,128)(2,1)}, bf16[750,384]{0,1:T(8,128)(2,1)S(1)}, u32[]{:S(2)}) copy-start(bf16[750,384]{0,1:T(8,128)(2,1)S(1)} %copy.39) | copy-start | bytes 1728004
  364.1 20.3 %copy-start.8 = (bf16[1500,6,64]{0,2,1:T(8,128)(2,1)}, bf16[1500,6,64]{0,2,1:T(8,128)(2,1)S(1)}, u32[]{:S(2)}) copy-start(bf16[1500,6,64]{0,2,1:T(8,128)(2,1)S(1)} %reshape.551) | copy-start | bytes 3456004
  408.0 13.9 %copy-start.39 = (bf16[6,64,750]{2,1,0:T(8,128)(2,1)}, bf16[6,64,750]{2,1,0:T(8,128)(2,1)S(1)}, u32[]{:S(2)}) copy-start(bf16[6,64,750]{2,1,0:T(8,128)(2,1)S(1)} %fusion.43) | copy-start | bytes 1728004
  466.3 22.8 %copy-start.22 = (bf16[750,384]{0,1:T(8,128)(2,1)S(1)}, bf16[750,384]{0,1:T(8,128)(2,1)}, u32[]{:S(2)}) copy-start(bf16[750,384]{0,1:T(8,128)(2,1)} %copy-done.21) | copy-start | bytes 1728004
  497.6 232.2 %all-reduce.19.cloned.1.call-start = ((), (), s32[]{:S(2)}) async-start(), calls=%async_computation.8 | async-start | bytes 4718592
  518.9 50.5 %copy-start.67 = (f32[750]{0:T(1024)S(1)}, f32[750]{0:T(1024)}, u32[]{:S(2)}) copy-start(f32[750]{0:T(1024)} %copy-done.66) | copy-start | bytes 9004
  518.9 50.5 %copy-start.76 = (f32[750]{0:T(1024)S(1)}, f32[750]{0:T(1024)}, u32[]{:S(2)}) copy-start(f32[750]{0:T(1024)} %copy-done.75) | copy-start | bytes 9004
  518.9 50.5 %copy-start.90 = (f32[384]{0:T(512)S(1)}, f32[384]{0:T(512)}, u32[]{:S(2)}) copy-start(f32[384]{0:T(512)} %copy-done.89) | copy-start | bytes 4612
  627.7 22.8 %copy-start.20 = (bf16[750,384]{0,1:T(8,128)(2,1)S(1)}, bf16[750,384]{0,1:T(8,128)(2,1)}, u32[]{:S(2)}) copy-start(bf16[750,384]{0,1:T(8,128)(2,1)} %copy-done.19) | copy-start | bytes 1728004
  660.9 270.2 %all-reduce.17.cloned.1.call-start = ((), (), s32[]{:S(2)}) async-start(), calls=%async_computation.7 | async-start | bytes 14196736
  671.0 13.2 %copy-start.108 = (bf16[384]{0:T(512)(128)(2,1)S(1)}, bf16[384]{0:T(512)(128)(2,1)}, u32[]{:S(2)}) copy-start(bf16[384]{0:T(512)(128)(2,1)} %get-tuple-element.84) | copy-start | bytes 2308
  671.0 16.0 %copy-start.36 = (bf16[750,384]{0,1:T(8,128)(2,1)S(1)}, bf16[750,384]{0,1:T(8,128)(2,1)}, u32[]{:S(2)}) copy-start(bf16[750,384]{0,1:T(8,128)(2,1)} %copy-done.35) | copy-start | bytes 1728004
  675.1 16.4 %copy-start.101 = (bf16[384]{0:T(512)(128)(2,1)S(1)}, bf16[384]{0:T(512)(128)(2,1)}, u32[]{:S(2)}) copy-start(bf16[384]{0:T(512)(128)(2,1)} %get-tuple-element.145) | copy-start | bytes 2308
  675.1 17.9 %copy-start.107 = (bf16[384]{0:T(512)(128)(2,1)S(1)}, bf16[384]{0:T(512)(128)(2,1)}, u32[]{:S(2)}) copy-start(bf16[384]{0:T(512)(128)(2,1)} %get-tuple-element.102) | copy-start | bytes 2308
  675.1 20.7 %copy-start.102 = (bf16[1536]{0:T(1024)(128)(2,1)S(1)}, bf16[1536]{0:T(1024)(128)(2,1)}, u32[]{:S(2)}) copy-start(bf16[1536]{0:T(1024)(128)(2,1)} %get-tuple-element.187) | copy-start | bytes 9220
  675.1 21.3 %copy-start.7 = (bf16[1500,6,64]{0,2,1:T(8,128)(2,1)S(1)}, bf16[1500,6,64]{0,2,1:T(8,128)(2,1)}, u32[]{:S(2)}) copy-start(bf16[1500,6,64]{0,2,1:T(8,128)(2,1)} %copy-done.6) | copy-start | bytes 3456004
  705.5 27.4 %copy-start.2 = (bf16[1,750,384]{2,1,0:T(8,128)(2,1)S(1)}, bf16[1,750,384]{2,1,0:T(8,128)(2,1)}, u32[]{:S(2)}) copy-start(bf16[1,750,384]{2,1,0:T(8,128)(2,1)} %param.5) | copy-start | bytes 1728004
  705.5 27.4 %copy-start.30 = (bf16[384,1152]{1,0:T(8,128)(2,1)S(1)}, bf16[384,1152]{1,0:T(8,128)(2,1)}, u32[]{:S(2)}) copy-start(bf16[384,1152]{1,0:T(8,128)(2,1)} %copy-done.29) | copy-start | bytes 2654212
  705.5 27.4 %copy-start.59 = (f32[750]{0:T(1024)S(1)}, f32[750]{0:T(1024)}, u32[]{:S(2)}) copy-start(f32[750]{0:T(1024)} %copy-done.58) | copy-start | bytes 9004
  705.5 27.4 %copy-start.84 = (f32[384]{0:T(512)S(1)}, f32[384]{0:T(512)}, u32[]{:S(2)}) copy-start(f32[384]{0:T(512)} %copy-done.83) | copy-start | bytes 4612
  742.6 14.2 %copy-start.109 = (bf16[384]{0:T(512)(128)(2,1)S(1)}, bf16[384]{0:T(512)(128)(2,1)}, u32[]{:S(2)}) copy-start(bf16[384]{0:T(512)(128)(2,1)} %get-tuple-element.90) | copy-start | bytes 2308
  742.6 15.6 %copy-start.104 = (bf16[384]{0:T(512)(128)(2,1)S(1)}, bf16[384]{0:T(512)(128)(2,1)}, u32[]{:S(2)}) copy-start(bf16[384]{0:T(512)(128)(2,1)} %get-tuple-element.141) | copy-start | bytes 2308
  742.6 17.0 %copy-start.103 = (bf16[1536]{0:T(1024)(128)(2,1)S(1)}, bf16[1536]{0:T(1024)(128)(2,1)}, u32[]{:S(2)}) copy-start(bf16[1536]{0:T(1024)(128)(2,1)} %get-tuple-element.189) | copy-start | bytes 9220
  760.2 361.6 %all-reduce.15.cloned.1.call-start = ((), (), s32[]{:S(2)}) async-start(), calls=%async_computation.6 | async-start | bytes 14192640 | tf_op jit(solution)/shard_map/psum | solution.py:242
  933.5 17.4 %copy-start.53 = (bf16[1774080]{0:T(1024)(128)(2,1)S(1)}, bf16[1774080]{0:T(1024)(128)(2,1)}, u32[]{:S(2)}) copy-start(bf16[1774080]{0:T(1024)(128)(2,1)} %get-tuple-element.132) | copy-start | bytes 10644484
  974.5 147.4 %copy-start = (bf16[2,887040]{1,0:T(2,128)(2,1)S(1)}, bf16[2,887040]{1,0:T(2,128)(2,1)}, u32[]{:S(2)}) copy-start(bf16[2,887040]{1,0:T(2,128)(2,1)} %param.6) | copy-start | bytes 10644484
  (80 other events, 416.2 us)
Sparse Core Ops, SparseCore 0:
  16.1 91.3 all-gather.16
  109.6 89.4 all-gather.18
  201.1 22.4 all-gather.22
  225.6 22.4 all-gather.20
  311.7 22.4 all-gather.26
  336.2 22.4 all-gather.24
  497.7 68.6 all-reduce.20
  661.0 68.7 all-reduce.18
  760.4 170.6 all-reduce.16
  969.3 152.5 all-reduce.14
where the time goes:
time: 1180 us; the launch traced here: 1170 us
  waiting for transfers between devices  518 us (44%)
  local copies, waits for them, and re-layouts  267 us (23%)
  matrix products  231 us (20%)
  other arithmetic  133 us (11%)
  between operations  17.2 us (1%)
    unnamed x13, waiting for transfers between devices  233 us
    psum x1, waiting for transfers between devices, body(): layer_grads[layer_no] = lax.psum(group_part, 'rep')  146 us
    all_gather x2, waiting for transfers between devices, body(): full_vector = lax.all_gather(params[layer_no], 'shard', axis=0, tiled=True)  129 us
    slice x14, local copies, waits for them, and re-layouts, unpack(): pieces.append(vector[offset:offset + length].reshape(shape_of))  113 us
    convert_element_type x2, other arithmetic, attend_back(): (probs * (prob_grad - jnp.sum(probs * prob_grad, axis=-1, keepdims=True))...  45.5 us
    unnamed x263, local copies, waits for them, and re-layouts  45 us
    dot_general x2, matrix products, attend_back(): jnp.einsum('qhd,khd->hqk', grad_h, value_h, preferred_element_type=jnp.fl...  44.5 us
    sub x1, other arithmetic, body(): new_params = old_values - rate * step_size  37.6 us
  transfers between devices with their start and end apart: 10, of which 7 were waited for; matrix products, arithmetic and copies ran while one was open for 19% of the time, Pallas kernels for 0%

commit v1 on v0

v1 whole, which is shorter than its diff:
```python
from functools import partial

import jax
import jax.numpy as jnp
from jax import lax
from jax.experimental import pallas as pl
from jax.experimental.layout import Layout, with_layout_constraint
from jax.experimental.pallas import tpu as pltpu
from jax.sharding import PartitionSpec as P

D = 384
HEADS = 6
FF = 1536
LAYERS = 2
HD = D // HEADS
LANES = 128
T_QKV, T_O, T_UP, T_DOWN = 3 * D // LANES, D // LANES, FF // LANES, D // LANES
N_QKV, N_O, N_UP, N_DOWN = D * T_QKV, D * T_O, D * T_UP, FF * T_DOWN
N_SMALL = (8 * D + FF) // LANES
N_MAIN = N_O + N_UP + N_DOWN
N_ROWS = N_QKV + N_MAIN + N_SMALL
N_HALF = N_ROWS // 2
UP_BASE, DOWN_BASE = N_O, N_O + N_UP
MESH = pl.DeviceIdType.MESH
CHUNKS = 4
VECS = 16
FB = 384
RC = 256

ln_eps = 1e-05
rate = 0.01
beta_one = 0.9
beta_two = 0.95
adam_eps = 1e-08
decay = 0.1
fix_one = 1.0 - 0.9**3
fix_two = 1.0 - 0.95**3
LOG2E = 1.4426950408889634
SCALE2 = 0.125 * LOG2E
NEG = -1e30

f32 = jnp.float32
bf16 = jnp.bfloat16


def nn(left, right):
    return lax.dot_general(left, right, (((1,), (0,)), ((), ())), preferred_element_type=f32)


def nt(left, right):
    return lax.dot_general(left, right, (((1,), (1,)), ((), ())), preferred_element_type=f32)


def tn(left, right):
    return lax.dot_general(left, right, (((0,), (0,)), ((), ())), preferred_element_type=f32)


def stats(values):
    center = values - jnp.mean(values, axis=-1, keepdims=True)
    r = lax.rsqrt(jnp.mean(center * center, axis=-1, keepdims=True) + ln_eps)
    return center * r, r


def vec(vec_ref, row):
    return vec_ref[row : row + 1, :]


G1, G2, N1, BQ, BV, BO, N2, BD, BUP = range(9)


def each_chunk(rows, body):
    @pl.loop(0, rows // RC)
    def _(i):
        body(pl.ds(pl.multiple_of(i * RC, RC), RC))


def put_row(ref, row, value):
    for j in range(value.shape[1] // LANES):
        ref[row + j : row + j + 1, :] = value[:, j * LANES : (j + 1) * LANES]


def put_flat(ref, base, stride, value):
    for j in range(value.shape[1] // LANES):
        ref[pl.ds(base + j, value.shape[0], stride=stride), :] = value[:, j * LANES : (j + 1) * LANES]


def put_up(ref, shift, block, value):
    first = N_HALF - N_QKV - UP_BASE
    for j in range(value.shape[1] // LANES):
        tile = 3 * block + j
        piece = value[:, j * LANES : (j + 1) * LANES]
        cut = -(-(first - tile) // T_UP)
        ref[pl.ds(UP_BASE + tile, cut, stride=T_UP), :] = piece[:cut, :]
        ref[pl.ds(UP_BASE + tile + T_UP * cut + shift, D - cut, stride=T_UP), :] = piece[cut:, :]


def to_low(src, base, dst, step=64):
    rows = dst.shape[0]

    @pl.loop(0, rows // step)
    def _(i):
        at = pl.multiple_of(i * step, step)
        dst[pl.ds(at, step), :] = src[pl.ds(base + at, step), :].astype(bf16)


def unpack_kernel(flat_ref, *refs):
    outs, stage = refs[:-1], refs[-1]
    flat = flat_ref.reshape(2 * N_ROWS, LANES)
    start = 0
    for which, (tiles, count) in enumerate(
        ((T_QKV, N_QKV), (T_O, N_O), (T_UP, N_UP), (T_DOWN, N_DOWN))
    ):
        base = start

        @pl.loop(0, count // 192)
        def _(i):
            stage[pl.ds(pl.multiple_of(i * 384, 384), 384), :] = flat[
                pl.ds(pl.multiple_of(2 * base + i * 384, 128), 384), :
            ].astype(f32)

        @pl.loop(0, count // tiles // 128)
        def _(i):
            for layer in range(LAYERS):
                for j in range(tiles):
                    outs[5 * layer + which][
                        pl.ds(pl.multiple_of(i * 128, 128), 128), j * LANES : (j + 1) * LANES
                    ] = stage[pl.ds(i * (256 * tiles) + 2 * j + layer, 128, stride=2 * tiles), :].astype(bf16)

        start += count
    stage[0 : 2 * N_SMALL, :] = flat[2 * start : 2 * start + 2 * N_SMALL, :].astype(f32)
    for layer in range(LAYERS):
        for i in range(N_SMALL):
            row, j = i // 3, i % 3
            outs[5 * layer + 4][row : row + 1, j * LANES : (j + 1) * LANES] = stage[
                2 * i + layer : 2 * i + layer + 1, :
            ]


def gather_weights(w_rows):
    shapes = [
        jax.ShapeDtypeStruct((D, 3 * D), bf16),
        jax.ShapeDtypeStruct((D, D), bf16),
        jax.ShapeDtypeStruct((D, FF), bf16),
        jax.ShapeDtypeStruct((FF, D), bf16),
        jax.ShapeDtypeStruct((VECS, D), f32),
    ]
    sems = pltpu.SemaphoreType.DMA((2, CHUNKS))
    outs = pl.pallas_call(
        gather_kernel,
        out_shape=shapes * 2,
        in_specs=[pl.BlockSpec(memory_space=pl.ANY)],
        scratch_shapes=[
            pltpu.VMEM((N_ROWS, LAYERS, LANES), bf16),
            pltpu.VMEM((2 * N_UP, LANES), f32),
            pltpu.SemaphoreType.DMA,
            sems,
            pltpu.SemaphoreType.DMA((2,)),
            sems,
            sems,
            sems,
        ],
        compiler_params=pltpu.CompilerParams(vmem_limit_bytes=62 << 20, collective_id=0, has_side_effects=True),
        name="gather",
    )(w_rows)
    return outs[:5], outs[5:]


def reduce_grads(ranks, half_rows, pieces):
    bits = ranks.bit_length() - 1
    total = LAYERS * CHUNKS
    h = half_rows // CHUNKS // 2
    sems = pltpu.SemaphoreType.DMA((total, 2 * bits + 2))
    return pl.pallas_call(
        partial(reduce_kernel, ranks),
        out_shape=[jax.ShapeDtypeStruct((half_rows, LANES), bf16)] * 2,
        in_specs=[pl.BlockSpec(memory_space=pl.ANY)] * 6,
        out_specs=[pl.BlockSpec(memory_space=pl.ANY)] * 2,
        scratch_shapes=[
            pltpu.VMEM((LAYERS, 2 * half_rows, LANES), bf16),
            pltpu.VMEM((LAYERS, half_rows, LANES), bf16),
            pltpu.VMEM((total, 2, h, LANES), bf16),
            pltpu.VMEM((total, h, LANES), bf16),
            pltpu.VMEM((total, h, LANES), bf16),
            pltpu.SemaphoreType.DMA((2, 3)),
            pltpu.SemaphoreType.DMA((2,)),
            sems,
            sems,
        ],
        compiler_params=pltpu.CompilerParams(vmem_limit_bytes=62 << 20, collective_id=1, has_side_effects=True),
        name="reduce",
    )(*pieces)


def call(body, shapes, scratch, name):
    return pl.pallas_call(
        body,
        out_shape=shapes,
        scratch_shapes=scratch,
        compiler_params=pltpu.CompilerParams(vmem_limit_bytes=62 << 20),
        name=name,
    )


def qkv_forward(x_ref, wqkv_ref, vec_ref, q_ref, kv_ref):
    def chunk(rows):
        xhat, _ = stats(x_ref[rows, :].astype(f32))
        a = (xhat * vec(vec_ref, G1) + vec(vec_ref, N1)).astype(bf16)
        qkv = nn(a, wqkv_ref[...])
        q_ref[rows, :] = (qkv[:, :D] + vec(vec_ref, BQ)).astype(bf16)
        kv_ref[0, rows, :] = qkv[:, D : 2 * D].astype(bf16)
        kv_ref[1, rows, :] = (qkv[:, 2 * D :] + vec(vec_ref, BV)).astype(bf16)

    each_chunk(x_ref.shape[0], chunk)


def lane_half(shape, which):
    lane = lax.broadcasted_iota(jnp.int32, shape, 1)
    return (lane < HD) if which == 0 else (lane >= HD)


def pad_mask(scores, rows):
    pad = scores.shape[0] // 2
    edge = rows // 8 * 8
    keep = lax.broadcasted_iota(jnp.int32, (pad - edge, scores.shape[1]), 0) < rows - edge
    pieces = []
    for half in range(2):
        base = half * pad
        pieces.append(scores[base : base + edge, :])
        pieces.append(jnp.where(keep, scores[base + edge : base + pad, :], NEG))
    return jnp.concatenate(pieces, axis=0)


def pair(own_ref, oth_ref, which, cols):
    return jnp.concatenate([own_ref[which, :, cols], oth_ref[which, :, cols]], axis=0)


def head_scores(keys, q_pair, t, rows):
    q_one = jnp.where(lane_half(q_pair.shape, t), q_pair, jnp.zeros_like(q_pair))
    return pad_mask(nt(keys, q_one), rows), q_one


def attend(q_ref, own_ref, oth_ref, o_t_ref, lse_ref, rows):
    pad = q_ref.shape[0]
    for hp in range(HEADS // 2):
        cols = slice(hp * LANES, (hp + 1) * LANES)

        @pl.loop(0, pad // RC)
        def _(i):
            block = pl.ds(pl.multiple_of(i * RC, RC), RC)
            keys = pair(own_ref, oth_ref, 0, cols)
            values_t = pair(own_ref, oth_ref, 1, cols).T
            q_pair = q_ref[block, cols]
            for t in range(2):
                scores, _ = head_scores(keys, q_pair, t, rows)
                top = jnp.max(scores, axis=0, keepdims=True) * SCALE2
                probs = jnp.exp2(scores * SCALE2 - top).astype(bf16)
                ones = jnp.ones((16, 2 * pad), bf16)
                mixed = nn(jnp.concatenate([values_t[t * HD : (t + 1) * HD, :], ones], axis=0), probs)
                total = mixed[HD : HD + 1, :]
                head = 2 * hp + t
                o_t_ref[head * HD : (head + 1) * HD, block] = (mixed[:HD, :] / total).astype(bf16)
                lse_ref[head : head + 1, block] = top + jnp.log(total) * LOG2E


def out_forward(x_ref, o_t_ref, wo_ref, vec_ref, h1_ref):
    def chunk(rows):
        h1_ref[rows, :] = x_ref[rows, :].astype(f32) + tn(o_t_ref[:, rows], wo_ref[...]) + vec(vec_ref, BO)

    each_chunk(x_ref.shape[0], chunk)


def second_norm(h1_ref, vec_ref, a2_ref):
    def chunk(rows):
        xhat, _ = stats(h1_ref[rows, :])
        a2_ref[rows, :] = (xhat * vec(vec_ref, G2) + vec(vec_ref, N2)).astype(bf16)

    each_chunk(h1_ref.shape[0], chunk)


def mlp_forward(h1_ref, a2_ref, wup_ref, wdown_ref, vec_ref, x_ref):
    def chunk(rows):
        total = h1_ref[rows, :] + vec(vec_ref, BD)
        for b in range(FF // FB):
            cols = slice(b * FB, (b + 1) * FB)
            u = nn(a2_ref[rows, :], wup_ref[:, cols]) + vec(vec_ref, BUP + b)
            z = (u * (0.5 + 0.5 * lax.erf(u * 0.7071067811865476))).astype(bf16)
            total = total + nn(z, wdown_ref[cols, :])
        x_ref[rows, :] = total.astype(x_ref.dtype)

    each_chunk(h1_ref.shape[0], chunk)


def norm_backward(dy, xhat, r, gain):
    dyg = dy * gain
    inner = jnp.mean(dyg, axis=-1, keepdims=True)
    cross = jnp.mean(dyg * xhat, axis=-1, keepdims=True)
    return r * (dyg - inner - xhat * cross)


def column_sum(values):
    return jnp.sum(values.astype(f32), axis=0, keepdims=True)


def mlp_backward(shift, g_ref, h1_ref, a2_ref, wup_ref, wdown_ref, vec_ref, main_ref, da2_ref, dh1_ref, enc_ref):
    rows_all = g_ref.shape[0]
    small = N_MAIN + shift
    dy2 = g_ref[...].astype(bf16)
    put_row(main_ref, small + 21, column_sum(dy2))
    for b in range(FF // FB):
        cols = slice(b * FB, (b + 1) * FB)
        u = nn(a2_ref[...], wup_ref[:, cols]) + vec(vec_ref, BUP + b)
        cdf = 0.5 + 0.5 * lax.erf(u * 0.7071067811865476)
        z = (u * cdf).astype(bf16)
        slope = cdf + u * jnp.exp2(u * u * (-0.5 * LOG2E)) * 0.3989422804014327
        if enc_ref is not None:
            part = nn(z, wdown_ref[cols, :])
            if b == 0:
                enc_ref[...] = h1_ref[...] + vec(vec_ref, BD) + part
            else:
                enc_ref[...] += part
        put_flat(main_ref, DOWN_BASE + shift + T_DOWN * FB * b, T_DOWN, tn(z, dy2))
        du = (nt(dy2, wdown_ref[cols, :]) * slope).astype(bf16)
        put_row(main_ref, small + 24 + 3 * b, column_sum(du))
        put_up(main_ref, shift, b, tn(a2_ref[...], du))
        part = nt(du, wup_ref[:, cols])
        if b == 0:
            da2_ref[...] = part
        else:
            da2_ref[...] += part
    dgain = jnp.zeros((1, D), f32)
    dshift = jnp.zeros((1, D), f32)
    for i in range(rows_all // RC):
        rows = slice(i * RC, (i + 1) * RC)
        xhat, r = stats(h1_ref[rows, :])
        dy = da2_ref[rows, :]
        dgain += column_sum(dy * xhat)
        dshift += column_sum(dy)
        dh1_ref[rows, :] = g_ref[rows, :].astype(f32) + norm_backward(dy, xhat, r, vec(vec_ref, G2))
    put_row(main_ref, small + 3, dgain)
    put_row(main_ref, small + 18, dshift)


def out_backward(shift, dh1_ref, o_t_ref, wo_ref, main_ref, do_ref, delta_ref):
    dy1 = dh1_ref[...].astype(bf16)
    put_row(main_ref, N_MAIN + shift + 15, column_sum(dy1))
    put_flat(main_ref, 0, T_O, nn(o_t_ref[...], dy1))
    do_ref[...] = nt(dy1, wo_ref[...]).astype(bf16)
    do_t = nt(wo_ref[...], dy1).astype(bf16).astype(f32)
    prod = do_t * o_t_ref[...].astype(f32)
    for h in range(HEADS):
        delta_ref[h : h + 1, :] = jnp.sum(prod[h * HD : (h + 1) * HD, :], axis=0, keepdims=True)


def attend_backward(q_ref, own_ref, oth_ref, lse_ref, do_ref, delta_ref, dq_ref, dkv_own_ref, dkv_oth_ref,
                    dq_t_ref, dk_ref, dv_ref, rows):
    pad = q_ref.shape[0]
    for hp in range(HEADS // 2):
        cols = slice(hp * LANES, (hp + 1) * LANES)
        dk_ref[...] = jnp.zeros_like(dk_ref)
        dv_ref[...] = jnp.zeros_like(dv_ref)

        @pl.loop(0, pad // RC)
        def _(i):
            block = pl.ds(pl.multiple_of(i * RC, RC), RC)
            keys = pair(own_ref, oth_ref, 0, cols)
            values = pair(own_ref, oth_ref, 1, cols)
            keys_t = keys.T
            q_pair = q_ref[block, cols]
            do_pair = do_ref[block, cols]
            for t in range(2):
                head = 2 * hp + t
                scores, q_one = head_scores(keys, q_pair, t, rows)
                do_one = jnp.where(lane_half(do_pair.shape, t), do_pair, jnp.zeros_like(do_pair))
                probs = jnp.exp2(scores * SCALE2 - lse_ref[head : head + 1, block])
                dv_ref[...] += nn(probs.astype(bf16), do_one)
                ds = (probs * (nt(values, do_one) - delta_ref[head : head + 1, block])).astype(bf16)
                dk_ref[...] += nn(ds, q_one)
                dq_t_ref[t * HD : (t + 1) * HD, block] = nn(keys_t[t * HD : (t + 1) * HD, :], ds)

        dq_ref[:, cols] = (dq_t_ref[...] * 0.125).T.astype(bf16)
        dkv_own_ref[0, :, cols] = dk_ref[:pad, :] * 0.125
        dkv_own_ref[1, :, cols] = dv_ref[:pad, :]
        dkv_oth_ref[0, :, cols] = (dk_ref[pad:, :] * 0.125).astype(bf16)
        dkv_oth_ref[1, :, cols] = dv_ref[pad:, :].astype(bf16)


def qkv_backward(shift, x_ref, dq_ref, dkv_own_ref, dkv_in_ref, dh1_ref, wqkv_ref, vec_ref, gq_ref, tail_ref,
                 a_ref, da_ref, dx_ref):
    def first(rows):
        xhat, _ = stats(x_ref[rows, :].astype(f32))
        a_ref[rows, :] = (xhat * vec(vec_ref, G1) + vec(vec_ref, N1)).astype(bf16)

    each_chunk(x_ref.shape[0], first)
    for b in range(3):
        if b == 0:
            low = dq_ref[...]
        else:
            low = (dkv_own_ref[b - 1] + dkv_in_ref[b - 1].astype(f32)).astype(bf16)
        if b == 0:
            put_row(tail_ref, shift + 9, column_sum(low))
        if b == 2:
            put_row(tail_ref, shift + 12, column_sum(low))
        put_flat(gq_ref, 3 * b, T_QKV, tn(a_ref[...], low))
        part = nt(low, wqkv_ref[:, b * D : (b + 1) * D])
        if b == 0:
            da_ref[...] = part
        else:
            da_ref[...] += part
    dgain = jnp.zeros((1, D), f32)
    dshift = jnp.zeros((1, D), f32)
    for i in range(x_ref.shape[0] // RC):
        rows = slice(i * RC, (i + 1) * RC)
        xhat, r = stats(x_ref[rows, :].astype(f32))
        dy = da_ref[rows, :]
        dgain += column_sum(dy * xhat)
        dshift += column_sum(dy)
        dx_ref[rows, :] = (dh1_ref[rows, :] + norm_backward(dy, xhat, r, vec(vec_ref, G1))).astype(dx_ref.dtype)
    put_row(tail_ref, shift + 0, dgain)
    put_row(tail_ref, shift + 6, dshift)


def kernel_b(rows, x_ref, q_ref, own_ref, oth_ref, wo, wup, wdown, vec0, wqkv1, vec1,
             o_t, lse, h1, x1, q1, kv1, a2):
    attend(q_ref, own_ref, oth_ref, o_t, lse, rows)
    out_forward(x_ref, o_t, wo, vec0, h1)
    second_norm(h1, vec0, a2)
    mlp_forward(h1, a2, wup, wdown, vec0, x1)
    qkv_forward(x1, wqkv1, vec1, q1, kv1)


def main_start(main, shift):
    edge = N_HALF - N_QKV
    main[edge : edge + shift, :] = jnp.zeros((shift, LANES), f32)
    last = N_MAIN + shift
    main[last:, :] = jnp.zeros((main.shape[0] - last, LANES), f32)


def main_end(main, main_out, tail_out):
    to_low(main, 0, main_out)
    tail_out[...] = main[N_MAIN:, :]


def kernel_c(rows, shift, x_ref, q_ref, own_ref, oth_ref, wo, wup, wdown, vec1, cot,
             enc, dq, dkv_own, dkv_oth, dh1, main_out, tail_out,
             o_t, lse, h1, a2, enc32, main, da2, do, delta, dq_t, dk, dv):
    main_start(main, shift)
    attend(q_ref, own_ref, oth_ref, o_t, lse, rows)
    out_forward(x_ref, o_t, wo, vec1, h1)
    second_norm(h1, vec1, a2)
    mlp_backward(shift, cot, h1, a2, wup, wdown, vec1, main, da2, dh1, enc32)
    enc[...] = enc32[...].astype(bf16)
    out_backward(shift, dh1, o_t, wo, main, do, delta)
    main_end(main, main_out, tail_out)
    attend_backward(q_ref, own_ref, oth_ref, lse, do, delta, dq, dkv_own, dkv_oth, dq_t, dk, dv, rows)


def kernel_d(rows, shift, x1, dq1, dkv_own1, dkv_in1, dh11, wqkv1, vec1, tail1_in,
             q0, own0, oth0, o_t, lse, h1, wo, wup, wdown, vec0,
             gq1_out, tail1_out, dq, dkv_own, dkv_oth, dh1, main_out, tail_out,
             a, dx, gq1, tail1, main, da, do, delta, dq_t, dk, dv):
    tail1[...] = tail1_in[...]
    qkv_backward(shift, x1, dq1, dkv_own1, dkv_in1, dh11, wqkv1, vec1, gq1, tail1, a, da, dx)
    to_low(gq1, 0, gq1_out)
    tail1_out[...] = tail1[...].astype(bf16)
    main_start(main, shift)
    second_norm(h1, vec0, a)
    mlp_backward(shift, dx, h1, a, wup, wdown, vec0, main, da, dh1, None)
    out_backward(shift, dh1, o_t, wo, main, do, delta)
    main_end(main, main_out, tail_out)
    attend_backward(q0, own0, oth0, lse, do, delta, dq, dkv_own, dkv_oth, dq_t, dk, dv, rows)


def kernel_e(shift, x0, dq, dkv_own, dkv_in, dh1, wqkv, vec0, tail_in, gq_out, tail_out, dx, a, da, gq, tail):
    tail[...] = tail_in[...]
    qkv_backward(shift, x0, dq, dkv_own, dkv_in, dh1, wqkv, vec0, gq, tail, a, da, dx)
    to_low(gq, 0, gq_out)
    tail_out[...] = tail[...].astype(bf16)


def remote(src, dst, send, recv, where):
    copy = pltpu.make_async_remote_copy(
        src_ref=src, dst_ref=dst, send_sem=send, recv_sem=recv, device_id=where, device_id_type=MESH
    )
    copy.start()
    return copy


def meet(partners):
    barrier = pltpu.get_barrier_semaphore()
    for where in partners:
        pl.semaphore_signal(barrier, inc=1, device_id=where, device_id_type=MESH)
    pl.semaphore_wait(barrier, len(partners))


def gather_kernel(own_ref, *refs):
    outs, (both, stage, load, x_sems, tail_sems, core_sems, y_sems, far_sems) = refs[:10], refs[10:]
    s, r = lax.axis_index("shard"), lax.axis_index("rep")
    across, core, beside = {"shard": 1 - s}, {"rep": r ^ 1}, {"rep": r ^ 2}
    quarter = N_HALF // 4
    step = quarter // CHUNKS
    filling = pltpu.make_async_copy(own_ref, both.at[pl.ds(s * N_HALF, N_HALF)], load)
    filling.start()
    meet((across, core, beside))
    filling.wait()

    def part(half, q, c):
        return both.at[pl.ds(half * N_HALF + q * quarter + c * step, step)]

    def send(half, q, c, sems, where):
        ref = part(half, q, c)
        return remote(ref, ref, sems.at[0, c], sems.at[1, c], where)

    q = r % 4
    rest = both.at[pl.ds(s * N_HALF + 4 * quarter, N_HALF - 4 * quarter)]
    xs = [send(s, q, c, x_sems, across) for c in range(CHUNKS)]
    xs.append(remote(rest, rest, tail_sems.at[0], tail_sems.at[1], across))
    cores, ys, fars = [], [], []
    for c in range(CHUNKS + 1):
        if c < CHUNKS:
            xs[c].wait_recv()
            ys.append(send(1 - s, q, c, y_sems, beside))
            cores.append(send(1 - s, q, c, core_sems, core))
        if c > 0:
            ys[c - 1].wait_recv()
            fars.append(send(1 - s, q ^ 2, c - 1, far_sems, core))
    xs[CHUNKS].wait_recv()
    for copy in cores + fars:
        copy.wait_recv()
    for copy in xs + cores + ys + fars:
        copy.wait_send()
    unpack_kernel(both, *outs, stage)


def reduce_kernel(ranks, gq0, main0, tail0, gq1, main1, tail1, out0, out1,
                  acc, res, r_core, r_x, r_rep, load, store, send_sems, recv_sems):
    s, r = lax.axis_index("shard"), lax.axis_index("rep")
    bits = ranks.bit_length() - 1
    half_rows = res.shape[1]
    loads = []
    for layer, pieces in enumerate(((gq0, main0, tail0), (gq1, main1, tail1))):
        at = 0
        for k, piece in enumerate(pieces):
            copy = pltpu.make_async_copy(
                piece, acc.at[layer, pl.ds(at, piece.shape[0])], load.at[layer, k]
            )
            copy.start()
            loads.append(copy)
            at += piece.shape[0]
    across = {"shard": 1 - s}
    peers = [{"rep": r ^ (1 << b)} for b in range(bits)]
    meet([across] + peers)
    for copy in loads:
        copy.wait()
    n = half_rows // CHUNKS
    h = n // 2
    bit = [(r >> b) & 1 for b in range(bits)]
    stages = 2 * bits + 1

    def rows(at, size):
        return pl.ds(pl.multiple_of(at, 16), size)

    def add(layer, at, recv, out, out_at):
        step = 16
        while recv.shape[0] % (2 * step) == 0 and step < 128:
            step *= 2

        @pl.loop(0, recv.shape[0] // step)
        def _(i):
            total = acc[layer, rows(at + i * step, step), :].astype(f32) + recv[rows(i * step, step), :].astype(f32)
            out[layer, rows(out_at + i * step, step), :] = total.astype(bf16)

    def offset(level):
        return bit[0] * h + sum(bit[b] * (h >> b) for b in range(1, level + 1))

    def begin(ci, stage):
        layer, c = ci // CHUNKS, ci % CHUNKS
        base = c * n
        sems = lambda k: (send_sems.at[ci, stage + k], recv_sems.at[ci, stage + k])
        if stage == 0:
            out = []
            for half in range(2):
                src = acc.at[layer, rows(half * half_rows + base + (1 - bit[0]) * h, h)]
                out.append(remote(src, r_core.at[ci, half], *sems(0 if half == 0 else stages), peers[0]))
            return out
        if stage == 1:
            src = acc.at[layer, rows((1 - s) * half_rows + base + offset(0), h)]
            return [remote(src, r_x.at[ci], *sems(0), across)]
        if stage <= bits:
            b = stage - 1
            size = h >> b
            src = acc.at[layer, rows(s * half_rows + base + offset(b - 1) + (1 - bit[b]) * size, size)]
            return [remote(src, r_rep.at[ci, rows(h - 2 * size, size)], *sems(0), peers[b])]
        b = 2 * bits - stage
        ref = res.at[layer, rows(base + offset(b), h >> b)]
        return [remote(ref, ref, *sems(0), peers[b])]

    def finish(ci, stage, copies):
        layer, c = ci // CHUNKS, ci % CHUNKS
        base = c * n
        for copy in copies:
            copy.wait_recv()
        if stage == 0:
            for half in range(2):
                at = half * half_rows + base + offset(0)
                add(layer, at, r_core.at[ci, half], acc, at)
        elif stage == 1:
            at = s * half_rows + base + offset(0)
            add(layer, at, r_x.at[ci], acc, at)
        elif stage <= bits:
            b = stage - 1
            size = h >> b
            at = s * half_rows + base + offset(b)
            recv = r_rep.at[ci, rows(h - 2 * size, size)]
            if stage < bits:
                add(layer, at, recv, acc, at)
            else:
                add(layer, at, recv, res, base + offset(b))

    total = LAYERS * CHUNKS
    flying, everything = {}, []
    for tick in range(total + stages):
        for ci in range(total):
            stage = tick - ci
            if 0 < stage <= stages:
                finish(ci, stage - 1, flying.pop(ci))
            if 0 <= stage < stages:
                flying[ci] = begin(ci, stage)
                everything += flying[ci]
    for copy in everything:
        copy.wait_send()
    outs = [pltpu.make_async_copy(res.at[k], out, store.at[k]) for k, out in enumerate((out0, out1))]
    for copy in outs:
        copy.start()
    for copy in outs:
        copy.wait()


def adam_kernel(g0_ref, g1_ref, w_ref, one_ref, two_ref, g_out, p_out, one_out, two_out, w_stage):
    block = g0_ref.shape[0]
    flat = lambda ref: ref.reshape(LAYERS * block, LANES)
    w_stage[...] = flat(w_ref)[...].astype(f32)
    for layer, g_ref in enumerate((g0_ref, g1_ref)):
        for at in range(0, block, 64):
            rows = pl.ds(LAYERS * at + layer, 64, stride=LAYERS)
            grad = g_ref[at : at + 64, :].astype(f32)
            weight = w_stage[rows, :]
            one = beta_one * flat(one_ref)[rows, :] + (1.0 - beta_one) * grad
            two = beta_two * flat(two_ref)[rows, :] + (1.0 - beta_two) * grad * grad
            step = one / fix_one / (jnp.sqrt(two / fix_two) + adam_eps) + decay * weight
            flat(g_out)[rows, :] = grad
            flat(p_out)[rows, :] = weight - rate * step
            flat(one_out)[rows, :] = one
            flat(two_out)[rows, :] = two


def to_rows(array):
    view = array.reshape(LAYERS, -1, LANES)
    return with_layout_constraint(view, Layout(major_to_minor=(1, 0, 2))).transpose(1, 0, 2)


def from_rows(array):
    view = with_layout_constraint(array.transpose(1, 0, 2), Layout(major_to_minor=(1, 0, 2)))
    return view.reshape(LAYERS, -1)


def body(ranks, frames_in, params, moment_one, moment_two, cotangent):
    rows = frames_in.shape[1]
    pad = -(-rows // RC) * RC
    unit = 16 * ranks * CHUNKS
    half_rows = -(-N_HALF // unit) * unit
    shift = half_rows - N_HALF
    tail_rows = 2 * half_rows - N_QKV - N_MAIN

    def vm(shape, dtype):
        return pltpu.VMEM(shape, dtype)

    def sd(shape, dtype):
        return jax.ShapeDtypeStruct(shape, dtype)

    swap_pairs = []
    for s in range(2):
        for r in range(ranks):
            here = s * ranks + r
            swap_pairs.append((here, here if s == r % 2 else (1 - s) * ranks + (r ^ 1)))
    partner = [(r, r ^ 1) for r in range(ranks)]

    def swap(array):
        return lax.ppermute(array, ("shard", "rep"), swap_pairs)

    def exchange(array):
        return lax.ppermute(array, "rep", partner)

    x0 = swap(jnp.pad(frames_in[0], ((0, pad - rows), (0, 0))))
    cot = swap(jnp.pad(cotangent[0], ((0, pad - rows), (0, 0))))
    w_rows = to_rows(params)
    w0, w1 = gather_weights(w_rows)
    wqkv0, wo0, wup0, wdown0, vec0 = w0
    wqkv1, wo1, wup1, wdown1, vec1 = w1

    row_b = sd((pad, D), bf16)
    kv_b = sd((2, pad, D), bf16)
    kv_f = sd((2, pad, D), f32)
    row_f = sd((pad, D), f32)
    main_b = sd((N_MAIN, LANES), bf16)
    tail_f = sd((tail_rows, LANES), f32)
    tail_b = sd((tail_rows, LANES), bf16)
    gq_b = sd((N_QKV, LANES), bf16)
    main_s = vm((N_MAIN + tail_rows, LANES), f32)
    gq_s = vm((N_QKV, LANES), f32)
    tail_s = vm((tail_rows, LANES), f32)
    lse_f = sd((8, pad), f32)
    o_t_b = sd((D, pad), bf16)
    q0, kv0 = call(qkv_forward, [row_b, kv_b], [], "qkv0")(x0, wqkv0, vec0)
    kv0_in = exchange(kv0)
    o_t0, lse0, h10, x1, q1, kv1 = call(
        partial(kernel_b, rows), [o_t_b, lse_f, row_f, row_f, row_b, kv_b], [vm((pad, D), bf16)], "forward0"
    )(x0, q0, kv0, kv0_in, wo0, wup0, wdown0, vec0, wqkv1, vec1)
    kv1_in = exchange(kv1)
    attn_scratch = [
        vm((pad, D), bf16), vm((8, pad), f32), vm((LANES, pad), f32),
        vm((2 * pad, LANES), f32), vm((2 * pad, LANES), f32),
    ]
    enc, dq1, dkv1, dkv1_oth, dh11, main1, tail1 = call(
        partial(kernel_c, rows, shift), [row_b, row_b, kv_f, kv_b, row_f, main_b, tail_f],
        [vm((D, pad), bf16), vm((8, pad), f32), vm((pad, D), f32), vm((pad, D), bf16), vm((pad, D), f32),
         main_s, vm((pad, D), f32)] + attn_scratch, "middle1",
    )(x1, q1, kv1, kv1_in, wo1, wup1, wdown1, vec1, cot)
    dkv1_in = exchange(dkv1_oth)
    encoded = swap(enc[:rows])[None]
    gq1, tail1, dq0, dkv0, dkv0_oth, dh10, main0, tail0 = call(
        partial(kernel_d, rows, shift), [gq_b, tail_b, row_b, kv_f, kv_b, row_f, main_b, tail_f],
        [vm((pad, D), bf16), vm((pad, D), f32), gq_s, tail_s, main_s, vm((pad, D), f32)] + attn_scratch,
        "backward0",
    )(x1, dq1, dkv1, dkv1_in, dh11, wqkv1, vec1, tail1, q0, kv0, kv0_in, o_t0, lse0, h10, wo0, wup0, wdown0, vec0)
    dkv0_in = exchange(dkv0_oth)
    gq0, tail0, dx = call(
        partial(kernel_e, shift), [gq_b, tail_b, row_b],
        [vm((pad, D), bf16), vm((pad, D), f32), gq_s, tail_s], "last0"
    )(x0, dq0, dkv0, dkv0_in, dh10, wqkv0, vec0, tail0)
    frames_grad = swap(dx[:rows])[None]
    g0, g1 = reduce_grads(ranks, half_rows, (gq0, main0, tail0, gq1, main1, tail1))
    block = 640
    low = pl.BlockSpec((block, LANES), lambda i: (i, 0))
    spec = pl.BlockSpec((block, 2, LANES), lambda i: (i, 0, 0))
    row_shape = sd((N_HALF, 2, LANES), f32)
    grad, new_params, new_one, new_two = pl.pallas_call(
        adam_kernel, grid=(pl.cdiv(N_HALF, block),), in_specs=[low, low, spec, spec, spec], out_specs=[spec] * 4,
        out_shape=[row_shape] * 4, scratch_shapes=[vm((2 * block, LANES), f32)],
        compiler_params=pltpu.CompilerParams(vmem_limit_bytes=62 << 20), name="adam",
    )(g0, g1, w_rows, to_rows(moment_one), to_rows(moment_two))
    return (encoded, frames_grad, from_rows(grad), from_rows(new_params), from_rows(new_one), from_rows(new_two))


def solution(mesh):
    in_specs = (
        P("rep", "shard", None),
        P(None, "shard"),
        P(None, "shard"),
        P(None, "shard"),
        P("rep", "shard", None),
    )
    out_specs = (
        P("rep", "shard", None),
        P("rep", "shard", None),
        P(None, "shard"),
        P(None, "shard"),
        P(None, "shard"),
        P(None, "shard"),
    )
    return jax.shard_map(
        partial(body, mesh.shape["rep"]), mesh=mesh, in_specs=in_specs, out_specs=out_specs, check_vma=False
    )
```

time: 1180 us -> 354 us (0.30)
  waiting for transfers between devices: 518 us -> 14.2 us
  Pallas kernels: 0 us -> 309 us
  local copies, waits for them, and re-layouts: 267 us -> 9.86 us
  matrix products: 231 us -> 0 us
  other arithmetic: 133 us -> 0 us
  between operations: 17.2 us -> 0.98 us
  starting transfers between devices: 0.41 us -> 13.5 us
    pallas_call x0 -> x8, Pallas kernels: none -> 309 us  [the longest x1 86.1 us: reduce_grads(): pl.pallas_call(partial(reduce_kernel, ranks), out_shape=[jax.ShapeDtypeSt...]
    unnamed x13 -> x0, waiting for transfers between devices: 233 us -> none
    dot_general x36 -> x0, matrix products: 231 us -> none  [the longest x2 44.5 us: attend_back(): jnp.einsum('qhd,khd->hqk', grad_h, value_h, preferred_element_type=jnp.fl...]
    psum x1 -> x0, waiting for transfers between devices: 146 us -> none  [body(): layer_grads[layer_no] = lax.psum(group_part, 'rep')]
    all_gather x6 -> x0, waiting for transfers between devices: 139 us -> none  [the longest x2 129 us: body(): full_vector = lax.all_gather(params[layer_no], 'shard', axis=0, tiled=True)]
    slice x19 -> x2, local copies, waits for them, and re-layouts: 123 us -> 1.99 us  [the longest x1 1.12 us: body(): frames_grad = swap(dx[:rows])[None]]
    convert_element_type x12 -> x0, other arithmetic: 58.7 us -> none  [the longest x2 45.5 us: attend_back(): (probs * (prob_grad - jnp.sum(probs * prob_grad, axis=-1, keepdims=True))...]
    unnamed x263 -> x18, local copies, waits for them, and re-layouts: 45 us -> 6.69 us
  transfers between devices with their start and end apart: 10 -> 8, of which waited for: 7 -> 3; matrix products, arithmetic and copies ran while one was open for 19% -> 1% of each run, Pallas kernels for 0% -> 47%
where the time goes in v1:
time: 354 us; the launch traced here: 347 us
  Pallas kernels  309 us (87%)
  waiting for transfers between devices  14.2 us (4%)
  starting transfers between devices  13.5 us (4%)
  local copies, waits for them, and re-layouts  9.86 us (3%)
    pallas_call x1, Pallas kernels, reduce_grads(): pl.pallas_call(partial(reduce_kernel, ranks), out_shape=[jax.ShapeDtypeSt...  86.1 us
    pallas_call x1, Pallas kernels, body(): call(partial(kernel_c, rows, shift), [row_b, row_b, kv_f, kv_b, row_f, ma...  62.1 us
    pallas_call x1, Pallas kernels, body(): call(partial(kernel_d, rows, shift), [gq_b, tail_b, row_b, kv_f, kv_b, ro...  47.2 us
    pallas_call x1, Pallas kernels, gather_weights(): pl.pallas_call(gather_kernel, out_shape=shapes * 2, in_specs=[pl.BlockSpe...  44.8 us
    pallas_call x1, Pallas kernels, body(): call(partial(kernel_b, rows), [o_t_b, lse_f, row_f, row_f, row_b, kv_b],...  31.3 us
    pallas_call x1, Pallas kernels, body(): pl.pallas_call(adam_kernel, grid=(pl.cdiv(N_HALF, block),), in_specs=[low...  24.9 us
    ppermute x4, starting transfers between devices, swap(): return lax.ppermute(array, ('shard', 'rep'), swap_pairs)  13.1 us
    ppermute x4, waiting for transfers between devices, swap(): return lax.ppermute(array, ('shard', 'rep'), swap_pairs)  8.16 us
  transfers between devices with their start and end apart: 8, of which 3 were waited for; matrix products, arithmetic and copies ran while one was open for 1% of the time, Pallas kernels for 47%

profile of v1, /device:TPU:1, one launch (start us, length us, event | category | flops | bytes accessed | tf_op | source)
XLA Modules:
  0.0 347.2 jit_solution(11576979937016946339)
XLA Ops:
  0.6 1.1 pad.7
  1.8 4.5 %collective-permute-start = (bf16[768,384]{1,0:T(8,128)(2,1)S(1)}, bf16[768,384]{1,0:T(8,128)(2,1)S(1)}, u32[]{:S(2)}, u32[]{:S(2)}) collective-permute-start(bf16[768,384]{1,0:T(8,128)(2,1)S(1)} %pad.7), channel_id=1, source_target_pairs={{0,0},{1,16},{2,2},{3,18},{4,4},{5,20},{6,6},{7,22},{8,8},{9,24},{... | collective-permute-start | bytes 1769480 | tf_op jit(solution)/shard_map/ppermute | solution.py:688
  6.3 44.8 %gather.1 = (bf16[384,1152]{1,0:T(8,128)(2,1)}, bf16[384,384]{1,0:T(8,128)(2,1)}, bf16[384,1536]{1,0:T(8,128)(2,1)}, bf16[1536,384]{1,0:T(8,128)(2,1)}, f32[16,3...) custom-call(bf16[6930,2,128]{2,1,0:T(2,128)(2,1)} %bitcast.25), custom_call_target="tpu_custom_call" | custom-call | tf_op jit(solution)/shard_map/gather/pallas_call | solution.py:148
  51.0 0.0 collective-permute-done.x_ref.x0
  51.0 0.0 copy-start
  51.0 0.8 copy-done
  51.8 4.4 %qkv0.1 = (bf16[768,384]{1,0:T(8,128)(2,1)}, bf16[2,768,384]{2,1,0:T(8,128)(2,1)}) custom-call(bf16[768,384]{1,0:T(8,128)(2,1)} %copy-done, bf16[384,1152]{1,0:T(8,128)(2,1)} %get-tuple-element.48.wqkv_ref.wqkv, f32[16,384]{1,0:T(8,128)} %get-tuple-element.49.vec_ref.vec0), custom_call_target="tpu_custom_call" | custom-call | tf_op jit(solution)/shard_map/qkv0/pallas_call | solution.py:713
  56.3 0.1 collective-permute-start.1
  56.4 3.0 collective-permute-done.1.oth_ref.oth0
  59.4 0.0 copy-start.1
  59.4 1.0 copy-done.1
  60.4 0.0 copy-start.6
  60.4 31.3 %forward0.1 = (bf16[384,768]{1,0:T(8,128)(2,1)}, f32[8,768]{1,0:T(8,128)}, f32[768,384]{1,0:T(8,128)}, f32[768,384]{1,0:T(8,128)}, bf16[768,384]{1,0:T(8,128)(2,1)}, /*index=5*/bf16[2,768,384]{2,1,0:T(8,128)(2,1)}) custom-call(bf16[768,384]{1,0:T(8,128)(2,1)} %copy-done, bf16[768,384]{1,0:T(8,128)(2,1)} %get-tuple-element.50.q_ref.q0, ...), custom_call_target="tpu_custom_call" | custom-call | tf_op jit(solution)/shard_map/forward0/pallas_call | solution.py:715
  91.7 0.1 collective-permute-start.2
  91.8 0.0 copy-done.6
  91.8 0.1 pad.8
  91.9 3.0 collective-permute-start.3
  94.9 8.2 %collective-permute-done.3.cot = bf16[768,384]{1,0:T(8,128)(2,1)S(1)} collective-permute-done((bf16[768,384]{1,0:T(8,128)(2,1)S(1)}, bf16[768,384]{1,0:T(8,128)(2,1)S(1)}, u32[]{:S(2)}, u32[]{:S(2)}) %collective-permute-start.3) | collective-permute-done | bytes 589856 | tf_op jit(solution)/shard_map/ppermute | solution.py:688
  103.1 0.0 copy-start.5
  103.1 0.0 collective-permute-done.2.oth_ref
  103.1 0.0 copy-start.3
  103.1 0.8 copy-done.5
  103.9 0.4 copy-done.3
  104.3 62.1 %middle1.1 = (bf16[768,384]{1,0:T(8,128)(2,1)}, bf16[768,384]{1,0:T(8,128)(2,1)}, f32[2,768,384]{2,1,0:T(8,128)}, bf16[2,768,384]{2,1,0:T(8,128)(2,1)}, f32[768,...) custom-call(f32[768,384]{1,0:T(8,128)} %get-tuple-element.57.x_ref.x1, ...), custom_call_target="tpu_custom_call" | custom-call | tf_op jit(solution)/shard_map/middle1/pallas_call | solution.py:723
  166.3 0.0 collective-permute-start.5
  166.3 3.0 collective-permute-done.5.dkv_in1
  169.4 0.0 copy-start.2
  169.4 1.0 copy-done.2
  170.4 0.0 copy-start.7
  170.4 47.2 %backward0.1 = (bf16[3456,128]{1,0:T(8,128)(2,1)}, bf16[512,128]{1,0:T(8,128)(2,1)}, bf16[768,384]{1,0:T(8,128)(2,1)}, f32[2,768,384]{2,1,0:T(8,128)}, bf16[2,76...) custom-call(f32[768,384]{1,0:T(8,128)} %get-tuple-element.57.x_ref.x1, ...), custom_call_target="tpu_custom_call" | custom-call | tf_op jit(solution)/shard_map/backward0/pallas_call | solution.py:730
  217.6 0.2 collective-permute-start.6
  217.8 0.0 copy-done.7
  217.8 0.9 slice.6
  218.7 2.8 collective-permute-start.4
  221.6 0.0 collective-permute-done.6.dkv_in
  221.6 0.0 copy-start.4
  221.6 1.0 copy-done.4
  222.6 7.9 %last0.1 = (bf16[3456,128]{1,0:T(8,128)(2,1)}, bf16[512,128]{1,0:T(8,128)(2,1)}, bf16[768,384]{1,0:T(8,128)(2,1)}) custom-call(bf16[768,384]{1,0:T(8,128)(2,1)} %copy-done, bf16[768,384]{1,0:T(8,128)(2,1)} %get-tuple-element.72.dq, f32[2,768,384]{2,1,0:T(8,128)} %get-tuple-element.73.dkv_own, bf16[2,768,384]{2,1,0:T(8,128)(2,1)} %copy-done.4, ...), custom_call_target="tpu_custom_call" | custom-call | tf_op jit(solution)/shard_map/last0/pallas_call | solution.py:736
  230.5 1.1 slice.7
  231.6 2.7 collective-permute-start.7
  234.3 0.0 collective-permute-done.4
  234.3 86.1 %reduce.1 = (bf16[7168,128]{1,0:T(8,128)(2,1)}, bf16[7168,128]{1,0:T(8,128)(2,1)}) custom-call(bf16[3456,128]{1,0:T(8,128)(2,1)} %get-tuple-element.78.gq0, bf16[10368,128]{1,0:T(8,128)(2,1)} %get-tuple-element.79.main0, bf16[512,128]{1,0:T(8,128)(2,1)} %get-tuple-element.80.tail0, bf16[3456,128]{1,0:T(8,128)(2,1)} %get-tuple-element.81.gq1, ...), custom_call_target="tpu_custom_call" | custom-call | tf_op jit(solution)/shard_map/reduce/pallas_call | solution.py:173
  320.5 24.9 %adam.1 = (f32[6930,2,128]{2,1,0:T(2,128)}, f32[6930,2,128]{2,1,0:T(2,128)}, f32[6930,2,128]{2,1,0:T(2,128)}, f32[6930,2,128]{2,1,0:T(2,128)}) custom-call(bf16[7168,128]{1,0:T(8,128)(2,1)} %get-tuple-element.84.g0_ref, bf16[7168,128]{1,0:T(8,128)(2,1)} %get-tuple-element.85.g1_ref, bf16[6930,2,128]{2,1,0:T(2,128)(2,1)} %bitcast.26, ...), custom_call_target="tpu_custom_call" | custom-call | tf_op jit(solution)/shard_map/adam/pallas_call | solution.py:746
  345.3 0.0 collective-permute-done.7
  345.3 0.8 copy.13
  346.2 0.8 copy.14
Async XLA Ops:
  1.8 49.3 %collective-permute-start = (bf16[768,384]{1,0:T(8,128)(2,1)S(1)}, bf16[768,384]{1,0:T(8,128)(2,1)S(1)}, u32[]{:S(2)}, u32[]{:S(2)}) collective-permute-start(bf16[768,384]{1,0:T(8,128)(2,1)S(1)} %pad.7), channel_id=1, source_target_pairs={{0,0},{1,16},{2,2},{3,18},{4,4},{5,20},{6,6},{7,22},{8,8},{9,24},{... | collective-permute-start | bytes 1769480 | tf_op jit(solution)/shard_map/ppermute | solution.py:688
  51.0 0.8 copy-start
  56.3 3.1 collective-permute-start.1
  59.4 1.0 copy-start.1
  60.4 31.4 %copy-start.6 = (bf16[1,750,384]{2,1,0:T(8,128)(2,1)S(1)}, bf16[1,750,384]{2,1,0:T(8,128)(2,1)}, u32[]{:S(2)}) copy-start(bf16[1,750,384]{2,1,0:T(8,128)(2,1)} %param.9) | copy-start | bytes 1728004
  91.7 11.4 %collective-permute-start.2 = (bf16[2,768,384]{2,1,0:T(8,128)(2,1)}, bf16[2,768,384]{2,1,0:T(8,128)(2,1)S(1)}, u32[]{:S(2)}, u32[]{:S(2)}) collective-permute-start(bf16[2,768,384]{2,1,0:T(8,128)(2,1)} %get-tuple-element.59.own_ref), channel_id=1, source_target_pairs={{0,1},{1,0},{2,3},{3,2},{4,5},{5,4},{6,7},{7,6},{8,9},{9,8},{10,11... | collective-permute-start | bytes 3538952 | tf_op jit(solution)/shard_map/ppermute | solution.py:691
  91.9 11.2 %collective-permute-start.3 = (bf16[768,384]{1,0:T(8,128)(2,1)S(1)}, bf16[768,384]{1,0:T(8,128)(2,1)S(1)}, u32[]{:S(2)}, u32[]{:S(2)}) collective-permute-start(bf16[768,384]{1,0:T(8,128)(2,1)S(1)} %pad.8), channel_id=1, source_target_pairs={{0,0},{1,16},{2,2},{3,18},{4,4},{5,20},{6,6},{7,22},{8,8},{9,24},{... | collective-permute-start | bytes 1769480 | tf_op jit(solution)/shard_map/ppermute | solution.py:688
  103.1 0.8 copy-start.5
  103.1 1.2 copy-start.3
  166.3 3.1 collective-permute-start.5
  169.4 1.0 copy-start.2
  170.4 47.4 %copy-start.7 = (bf16[768,384]{1,0:T(8,128)(2,1)S(1)}, bf16[768,384]{1,0:T(8,128)(2,1)}, u32[]{:S(2)}) copy-start(bf16[768,384]{1,0:T(8,128)(2,1)} %get-tuple-element.63) | copy-start | bytes 1769476
  217.6 4.0 %collective-permute-start.6 = (bf16[2,768,384]{2,1,0:T(8,128)(2,1)}, bf16[2,768,384]{2,1,0:T(8,128)(2,1)S(1)}, u32[]{:S(2)}, u32[]{:S(2)}) collective-permute-start(bf16[2,768,384]{2,1,0:T(8,128)(2,1)} %get-tuple-element.74), channel_id=1, source_target_pairs={{0,1},{1,0},{2,3},{3,2},{4,5},{5,4},{6,7},{7,6},{8,9},{9,8},{10,11... | collective-permute-start | bytes 3538952 | tf_op jit(solution)/shard_map/ppermute | solution.py:691
  218.7 15.6 %collective-permute-start.4 = (bf16[750,384]{1,0:T(8,128)(2,1)}, bf16[750,384]{1,0:T(8,128)(2,1)S(1)}, u32[]{:S(2)}, u32[]{:S(2)}) collective-permute-start(bf16[750,384]{1,0:T(8,128)(2,1)} %slice.6), channel_id=1, source_target_pairs={{0,0},{1,16},{2,2},{3,18},{4,4},{5,20},{6,6},{7,22},{8,8},{9,24},{... | collective-permute-start | bytes 1728008 | tf_op jit(solution)/shard_map/ppermute | solution.py:688
  221.6 1.0 copy-start.4
  231.6 113.7 %collective-permute-start.7 = (bf16[750,384]{1,0:T(8,128)(2,1)S(1)}, bf16[750,384]{1,0:T(8,128)(2,1)S(1)}, u32[]{:S(2)}, u32[]{:S(2)}) collective-permute-start(bf16[750,384]{1,0:T(8,128)(2,1)S(1)} %slice.7), channel_id=1, source_target_pairs={{0,0},{1,16},{2,2},{3,18},{4,4},{5,20},{6,6},{7,22},{8,8},{9,24},{... | collective-permute-start | bytes 1728008 | tf_op jit(solution)/shard_map/ppermute | solution.py:688
